TPU v7x, 32 devices: a whole 2x2x4 slice. The times are simulated.
32 devices in a mesh: gx: 4 (over y, x), gy: 4 (over z), gz: 2 (over core).
Axes of the slice: x: 2, y: 2, z: 4, core: 2. Of those that a mesh axis runs over, the one named last changes fastest.
Arguments:
- gas_pos: float32 [3, 4, 4, 2, 2048], P(None, 'gx', 'gy', 'gz'), may hold values from 0 to 1
- gas_mass: float32 [4, 4, 2, 2048], P('gx', 'gy', 'gz'), may hold values from 0.2 to 5
- source_pos: float32 [3, 4, 4, 2, 2048], P(None, 'gx', 'gy', 'gz'), may hold values from 0 to 1
- source_radius: float32 [4, 4, 2, 2048], P('gx', 'gy', 'gz'), may hold values from 0.25 to 1
- source_yield: float32 [2, 4, 4, 2, 2048], P(None, 'gx', 'gy', 'gz'), may hold values from 1 to 30
- source_momentum: float32 [3, 4, 4, 2, 2048], P(None, 'gx', 'gy', 'gz'), may hold values from -180 to 180
- source_tiles: int32 [4, 4, 2, 16, 8], P('gx', 'gy', 'gz'), may hold values from 0 to 431, as said below
- source_count: int32 [4, 4, 2], P('gx', 'gy', 'gz'), may hold values from 1 to 2048, as said below
Outputs:
- gas_gain: float32 [5, 4, 4, 2, 2048], P(None, 'gx', 'gy', 'gz')
Inputs may be any that keep to these rules, and one draw needn't show every extreme that they name: `source_tiles`: the 8 tiles of one block lie one in each of the 8 domains around one corner of the block's domain (that domain among them), in increasing order. Over all blocks of one domain, at most 8 distinct listed tiles lie in any one neighbouring slot. `source_count`: some domain holds 2048 live sources in every draw.
All inputs are finite; a program needn't handle non-finite values.
Results may differ from a plain program's by a relative error of at most 0.0003.
Values sent between devices are 32-bit elements; how exact they have to be, the bound alone decides.
A program may use at most 64 MiB of HBM per device.

v0:
```python
import functools
import math

import jax
import jax.numpy as jnp
from jax import lax
from jax.experimental import pallas as pl
from jax.experimental.pallas import tpu as pltpu
from jax.sharding import PartitionSpec as P


def kinds(count):
    return min(count, 3)


def kind_of(offset, count):
    if count >= 3:
        return offset + 1
    if count == 2:
        return jnp.abs(offset)
    return offset * 0


def own_kind(count):
    return 1 if count >= 3 else 0


def steps_of(count):
    if count >= 3:
        return ((0, -1), (2, 1))
    return ((1, 1),) if count == 2 else ()


MESH = pl.DeviceIdType.MESH


def shifted(axis, count, step):
    return lax.rem(lax.axis_index(axis) + step + count, count)


def columns_of(sizes):
    nx, ny, _ = sizes
    choices_x = steps_of(nx) + ((own_kind(nx), 0),)
    choices_y = ((own_kind(ny), 0),) + steps_of(ny)
    return [
        ((i, j), {"gx": shifted("gx", nx, dx), "gy": shifted("gy", ny, dy)})
        for i, dx in choices_x
        for j, dy in choices_y
        if dx or dy
    ]


def cores_of(sizes):
    return [(k, {"gz": shifted("gz", sizes[2], dz)}) for k, dz in steps_of(sizes[2])]


def greet(sizes):
    barrier = pltpu.get_barrier_semaphore()
    peers = columns_of(sizes) + cores_of(sizes)
    for _, device in peers:
        pl.semaphore_signal(barrier, inc=1, device_id=device, device_id_type=MESH)
    if peers:
        pl.semaphore_wait(barrier, len(peers))


def facing(kind, count):
    return 2 - kind if count >= 3 else kind


def spread_kernel(sizes, pos, mass, near, local_sem, send_sem, recv_sem):
    nx, ny, nz = sizes
    own = tuple(own_kind(n) for n in sizes)

    def place(i, j, k):
        return (i * kinds(ny) + j) * kinds(nz) + k

    home = place(*own)
    first = pltpu.make_async_copy(pos, near.at[home, pl.ds(0, 3)], local_sem.at[0])
    second = pltpu.make_async_copy(mass, near.at[home, pl.ds(3, 1)], local_sem.at[1])
    first.start()
    second.start()
    greet(sizes)
    first.wait()
    second.wait()
    copies = {}

    def send(slot, there, device):
        target = place(*there)
        copy = pltpu.make_async_remote_copy(
            src_ref=near.at[place(*slot)],
            dst_ref=near.at[target],
            send_sem=send_sem.at[target],
            recv_sem=recv_sem.at[target],
            device_id=device,
            device_id_type=MESH,
        )
        copy.start()
        copies[there] = copy

    def to_cores(i, j):
        for k, device in cores_of(sizes):
            send((i, j, own[2]), (i, j, facing(k, nz)), device)

    columns = columns_of(sizes)
    for (i, j), device in columns:
        send(own, (facing(i, nx), facing(j, ny), own[2]), device)
    to_cores(own[0], own[1])
    across = [at for at, _ in columns if at[0] != own[0]]
    along = [at for at, _ in columns if at[0] == own[0]]
    for i, j in along + across:
        copies[i, j, own[2]].wait_recv()
        to_cores(i, j)
    for i, j in [own[:2]] + along + across:
        for k, _ in steps_of(nz):
            copies[i, j, k].wait_recv()
    for copy in copies.values():
        copy.wait_send()


def gather_kernel(sizes, moved, out, part, got_z, got, send_z, recv_z, send_sem, recv_sem):
    nx, ny, nz = sizes
    own = tuple(own_kind(n) for n in sizes)

    def place(i, j, k):
        return (i * kinds(ny) + j) * kinds(nz) + k

    greet(sizes)
    copies = []

    def send(src, dst, send_at, recv_at, device):
        copy = pltpu.make_async_remote_copy(
            src_ref=src, dst_ref=dst, send_sem=send_at, recv_sem=recv_at, device_id=device, device_id_type=MESH
        )
        copy.start()
        copies.append(copy)
        return copy

    columns = columns_of(sizes)
    order = [at for at, _ in columns] + [own[:2]]
    along_z, arriving = {}, {}
    for i, j in order:
        for k, device in cores_of(sizes):
            at = place(i, j, k)
            along_z[i, j, k] = send(moved.at[at], got_z.at[at], send_z.at[at], recv_z.at[at], device)

    def send_part(index):
        (i, j), device = columns[index]
        at = i * kinds(ny) + j
        arriving[at] = send(part.at[at], got.at[at], send_sem.at[at], recv_sem.at[at], device)

    for index, (i, j) in enumerate(order):
        total = moved[place(i, j, own[2])]
        for k, _ in steps_of(nz):
            along_z[i, j, k].wait_recv()
            total = total + got_z[place(i, j, k)]
        if index < len(columns):
            part[i * kinds(ny) + j] = total
        if index:
            send_part(index - 1)
    for at in reversed(list(arriving)):
        arriving[at].wait_recv()
        total = total + got[at]
    out[...] = total
    for copy in copies:
        copy.wait_send()


def split3(value):
    first = value.astype(jnp.bfloat16).astype(jnp.float32)
    rest = value - first
    second = rest.astype(jnp.bfloat16).astype(jnp.float32)
    return first, second, rest - second


def rows_of(rows):
    at = lax.broadcasted_iota(jnp.int32, (8, 128), 0)
    out = jnp.zeros((8, 128), jnp.float32)
    for i, row in enumerate(rows):
        out = jnp.where(at == i, row, out)
    return out


def deposit_kernel(sizes, tiles_each, unroll, table, count, near, pos, radius, yields, momentum, out, acc):
    blocks, listed = pos.shape[1], table.shape[1]
    slots = near.shape[0]
    nx, ny, nz = sizes
    acc[...] = jnp.zeros_like(acc)
    live_count = count[0]
    lane = lax.broadcasted_iota(jnp.int32, (1, 128), 1)

    def one_block(b):
        row = pl.ds(b, 1)
        r = radius[row, :]
        inv = 1.0 / (r * r)
        sx, sy, sz = (pos[k, row, :] - 0.5 for k in range(3))
        left = rows_of(
            [-2.0 * inv * sx, -2.0 * inv * sy, -2.0 * inv * sz, inv, 1.0 + inv * (sx * sx + sy * sy + sz * sz)]
        )
        a1, a2, a3 = split3(left)
        lhs = jnp.concatenate([a1, a1, a2, a2, a1, a3], axis=0).T.astype(jnp.bfloat16)
        norm_acc = jnp.zeros((128, 128), jnp.float32)
        high, low, places = [], [], []
        for j in range(listed):
            tile_id = table[b, j]
            slot, tile = tile_id // tiles_each, tile_id % tiles_each
            a, bb, c = slot // 9 - 1, slot // 3 % 3 - 1, slot % 3 - 1
            place = (kind_of(a, nx) * kinds(ny) + kind_of(bb, ny)) * kinds(nz) + kind_of(c, nz)
            places.append(place * tiles_each + tile)
            at = pl.ds(tile, 1)
            gx = near[place, 0, at, :] + (a.astype(jnp.float32) - 0.5)
            gy = near[place, 1, at, :] + (bb.astype(jnp.float32) - 0.5)
            gz = near[place, 2, at, :] + (c.astype(jnp.float32) - 0.5)
            mass = near[place, 3, at, :]
            b1, b2, b3 = split3(rows_of([gx, gy, gz, gx * gx + gy * gy + gz * gz, jnp.ones_like(gx)]))
            rhs = jnp.concatenate([b1, b2, b1, b2, b3, b1], axis=0).astype(jnp.bfloat16)
            u = jnp.dot(lhs, rhs, preferred_element_type=jnp.float32)
            w = 1.0 / (u * u)
            norm_acc = norm_acc + w * mass
            w1 = w.astype(jnp.bfloat16)
            high.append(w1)
            low.append((w - w1.astype(jnp.float32)).astype(jnp.bfloat16))
        norm = jnp.sum(norm_acc.T, axis=0, keepdims=True)
        live = jnp.where(b * 128 + lane < live_count, 1.0, 0.0)
        scale = live / norm
        loads = rows_of(
            [yields[0, row, :], momentum[0, row, :], momentum[1, row, :], momentum[2, row, :], yields[1, row, :]]
        )
        c1, c2, c3 = split3(loads * scale)
        coef = jnp.concatenate([c1, c2, c3, jnp.zeros_like(c1)], axis=0).astype(jnp.bfloat16)
        for j in range(listed):
            hi = jnp.dot(coef, high[j], preferred_element_type=jnp.float32)
            lo = jnp.dot(coef[0:16], low[j], preferred_element_type=jnp.float32)
            moved = hi[0:8] + (hi[8:16] + (hi[16:24] + (lo[0:8] + lo[8:16])))
            start = pl.multiple_of(places[j] * 8, 8)
            acc[pl.ds(start, 8), :] = acc[pl.ds(start, 8), :] + moved

    def step(i, carry):
        for k in range(unroll):
            one_block(i * unroll + k)
        return carry

    used = jnp.minimum((live_count + 127) // 128, blocks)
    lax.fori_loop(0, (used + unroll - 1) // unroll, step, 0)
    for slot in range(slots):
        for q in range(5):
            out[slot, q] = acc[pl.ds(slot * tiles_each * 8 + q, tiles_each, stride=8), :]


def local(sizes, gas_pos, gas_mass, source_pos, source_radius, source_yield, source_momentum, source_tiles, source_count):
    gas_size = gas_pos.shape[-1]
    tiles = gas_size // 128
    blocks = source_pos.shape[-1] // 128
    listed = source_tiles.shape[-1]
    nx, ny, nz = sizes
    slots = kinds(nx) * kinds(ny) * kinds(nz)
    vmem = pl.BlockSpec(memory_space=pltpu.VMEM)
    near = pl.pallas_call(
        functools.partial(spread_kernel, sizes),
        out_shape=jax.ShapeDtypeStruct((slots, 4, tiles, 128), jnp.float32),
        in_specs=[vmem, vmem],
        out_specs=vmem,
        scratch_shapes=[
            pltpu.SemaphoreType.DMA((2,)),
            pltpu.SemaphoreType.DMA((slots,)),
            pltpu.SemaphoreType.DMA((slots,)),
        ],
        compiler_params=pltpu.CompilerParams(collective_id=0, has_side_effects=True),
    )(gas_pos.reshape(3, tiles, 128), gas_mass.reshape(1, tiles, 128))
    unroll = math.gcd(blocks, 4)
    smem = pl.BlockSpec(memory_space=pltpu.SMEM)
    moved = pl.pallas_call(
        functools.partial(deposit_kernel, sizes, tiles, unroll),
        out_shape=jax.ShapeDtypeStruct((slots, 5, tiles, 128), jnp.float32),
        in_specs=[smem, smem] + [vmem] * 5,
        out_specs=vmem,
        scratch_shapes=[pltpu.VMEM((slots * tiles * 8, 128), jnp.float32)],
    )(
        source_tiles.reshape(blocks, listed),
        source_count.reshape(1),
        near,
        source_pos.reshape(3, blocks, 128),
        source_radius.reshape(blocks, 128),
        source_yield.reshape(2, blocks, 128),
        source_momentum.reshape(3, blocks, 128),
    )
    piece = (5, tiles, 128)
    sides = kinds(nx) * kinds(ny)
    gain = pl.pallas_call(
        functools.partial(gather_kernel, sizes),
        out_shape=jax.ShapeDtypeStruct(piece, jnp.float32),
        in_specs=[vmem],
        out_specs=vmem,
        scratch_shapes=[
            pltpu.VMEM((sides, *piece), jnp.float32),
            pltpu.VMEM((slots, *piece), jnp.float32),
            pltpu.VMEM((sides, *piece), jnp.float32),
            pltpu.SemaphoreType.DMA((slots,)),
            pltpu.SemaphoreType.DMA((slots,)),
            pltpu.SemaphoreType.DMA((sides,)),
            pltpu.SemaphoreType.DMA((sides,)),
        ],
        compiler_params=pltpu.CompilerParams(collective_id=1, has_side_effects=True),
    )(moved)
    return gain.reshape(5, 1, 1, 1, gas_size)


def solution(mesh):
    sizes = (mesh.shape["gx"], mesh.shape["gy"], mesh.shape["gz"])
    in_specs = (
        P(None, "gx", "gy", "gz", None),
        P("gx", "gy", "gz", None),
        P(None, "gx", "gy", "gz", None),
        P("gx", "gy", "gz", None),
        P(None, "gx", "gy", "gz", None),
        P(None, "gx", "gy", "gz", None),
        P("gx", "gy", "gz", None, None),
        P("gx", "gy", "gz"),
    )
    out_specs = P(None, "gx", "gy", "gz", None)
    return jax.shard_map(
        functools.partial(local, sizes), mesh=mesh, in_specs=in_specs, out_specs=out_specs, check_vma=False
    )
```

profile of v0, /device:TPU:0, one launch (start us, length us, event | category | flops | bytes accessed | tf_op | source)
XLA Modules:
  0.0 43.3 jit_solution(15375718909010874603)
XLA Ops:
  0.7 0.0 copy-start
  0.7 0.7 %copy-done = s32[1,1,1,16,8]{3,4,2,1,0:T(8,128)S(1)} copy-done((s32[1,1,1,16,8]{3,4,2,1,0:T(8,128)S(1)}, s32[1,1,1,16,8]{3,4,2,1,0:T(8,128)}, u32[]{:S(2)}) %copy-start) | copy-done | bytes 536
  1.3 0.7 %copy.11.table = s32[16,8]{1,0:T(8,128)} copy(s32[16,8]{0,1:T(8,128)S(1)} %bitcast.17) | data formatting | bytes 1024 | tf_op jit(solution)/shard_map/reshape | solution.py:278
  2.0 15.3 %shard_map.82.near = f32[18,4,16,128]{3,2,1,0:T(8,128)} custom-call(f32[3,16,128]{2,1,0:T(8,128)} %bitcast.11, f32[1,16,128]{2,1,0:T(8,128)} %bitcast.15), custom_call_target="tpu_custom_call" | custom-call | tf_op jit(solution)/shard_map/pallas_call | solution.py:257
  17.3 8.8 %shard_map.83.moved = f32[18,5,16,128]{3,2,1,0:T(8,128)} custom-call(s32[16,8]{1,0:T(8,128)} %copy.11.table, s32[1]{0:T(128)} %bitcast.9.count, f32[18,4,16,128]{3,2,1,0:T(8,128)} %shard_map.82.near, f32[3,16,128]{2,1,0:T(8,128)} %bitcast.12, f32[16,128]{1,0:T(8,128)} %bitcast.16, f32[2,16,128]{2,1,0:T(8,128)} %bitcast.14, f32[3,16,128]{2,1,0:T(8,128)} %bitcast.13), custom_call_target="tpu_custom_call" | custom-call | tf_op jit(solution)/shard_map/pallas_call | solution.py:271
  26.1 15.8 %shard_map.84 = f32[5,16,128]{2,1,0:T(8,128)} custom-call(f32[18,5,16,128]{3,2,1,0:T(8,128)} %shard_map.83.moved), custom_call_target="tpu_custom_call" | custom-call | tf_op jit(solution)/shard_map/pallas_call | solution.py:288
  41.9 1.4 %copy.15 = f32[5,1,1,1,2048]{4,3,2,1,0:T(1,128)} copy(f32[5,1,1,1,2048]{4,3,2,1,0:T(1,128)} %bitcast.10) | data formatting | bytes 81920
Async XLA Ops:
  0.7 0.7 %copy-start = (s32[1,1,1,16,8]{3,4,2,1,0:T(8,128)S(1)}, s32[1,1,1,16,8]{3,4,2,1,0:T(8,128)}, u32[]{:S(2)}) copy-start(s32[1,1,1,16,8]{3,4,2,1,0:T(8,128)} %param.14) | copy-start | bytes 1540
where the time goes:
time: 43.6 us; the launch traced here: 43.3 us
  Pallas kernels  39.9 us (92%)
  local copies, waits for them, and re-layouts  2.75 us (6%)
  between operations  0.68 us (2%)
    pallas_call x1, Pallas kernels, local(): pl.pallas_call(functools.partial(gather_kernel, sizes), out_shape=jax.Sha...  15.8 us
    pallas_call x1, Pallas kernels, local(): pl.pallas_call(functools.partial(spread_kernel, sizes), out_shape=jax.Sha...  15.3 us
    pallas_call x1, Pallas kernels, local(): pl.pallas_call(functools.partial(deposit_kernel, sizes, tiles, unroll), o...  8.8 us
    unnamed x3, local copies, waits for them, and re-layouts  2.08 us

commit v1 on v0

--- a/solution.py
+++ b/solution.py
@@ -32,6 +32,7 @@
 
 
 MESH = pl.DeviceIdType.MESH
+LIMIT = 24 * 1024 * 1024
 
 
 def shifted(axis, count, step):
@@ -181,7 +182,7 @@
 
 
 def deposit_kernel(sizes, tiles_each, unroll, table, count, near, pos, radius, yields, momentum, out, acc):
-    blocks, listed = pos.shape[1], table.shape[1]
+    blocks, listed = pos.shape[1], table.shape[0]
     slots = near.shape[0]
     nx, ny, nz = sizes
     acc[...] = jnp.zeros_like(acc)
@@ -201,7 +202,7 @@
         norm_acc = jnp.zeros((128, 128), jnp.float32)
         high, low, places = [], [], []
         for j in range(listed):
-            tile_id = table[b, j]
+            tile_id = table[j, b]
             slot, tile = tile_id // tiles_each, tile_id % tiles_each
             a, bb, c = slot // 9 - 1, slot // 3 % 3 - 1, slot % 3 - 1
             place = (kind_of(a, nx) * kinds(ny) + kind_of(bb, ny)) * kinds(nz) + kind_of(c, nz)
@@ -256,7 +257,7 @@
     vmem = pl.BlockSpec(memory_space=pltpu.VMEM)
     near = pl.pallas_call(
         functools.partial(spread_kernel, sizes),
-        out_shape=jax.ShapeDtypeStruct((slots, 4, tiles, 128), jnp.float32),
+        out_shape=pltpu.VMEM((slots, 4, tiles, 128), jnp.float32),
         in_specs=[vmem, vmem],
         out_specs=vmem,
         scratch_shapes=[
@@ -264,18 +265,19 @@
             pltpu.SemaphoreType.DMA((slots,)),
             pltpu.SemaphoreType.DMA((slots,)),
         ],
-        compiler_params=pltpu.CompilerParams(collective_id=0, has_side_effects=True),
+        compiler_params=pltpu.CompilerParams(collective_id=0, has_side_effects=True, vmem_limit_bytes=LIMIT),
     )(gas_pos.reshape(3, tiles, 128), gas_mass.reshape(1, tiles, 128))
     unroll = math.gcd(blocks, 4)
     smem = pl.BlockSpec(memory_space=pltpu.SMEM)
     moved = pl.pallas_call(
         functools.partial(deposit_kernel, sizes, tiles, unroll),
-        out_shape=jax.ShapeDtypeStruct((slots, 5, tiles, 128), jnp.float32),
+        out_shape=pltpu.VMEM((slots, 5, tiles, 128), jnp.float32),
         in_specs=[smem, smem] + [vmem] * 5,
         out_specs=vmem,
         scratch_shapes=[pltpu.VMEM((slots * tiles * 8, 128), jnp.float32)],
+        compiler_params=pltpu.CompilerParams(vmem_limit_bytes=LIMIT),
     )(
-        source_tiles.reshape(blocks, listed),
+        source_tiles.reshape(blocks, listed).T,
         source_count.reshape(1),
         near,
         source_pos.reshape(3, blocks, 128),
@@ -299,7 +301,7 @@
             pltpu.SemaphoreType.DMA((sides,)),
             pltpu.SemaphoreType.DMA((sides,)),
         ],
-        compiler_params=pltpu.CompilerParams(collective_id=1, has_side_effects=True),
+        compiler_params=pltpu.CompilerParams(collective_id=1, has_side_effects=True, vmem_limit_bytes=LIMIT),
     )(moved)
     return gain.reshape(5, 1, 1, 1, gas_size)
 

time: 43.6 us -> 38 us (0.87)
  Pallas kernels: 39.9 us -> 34.6 us
  local copies, waits for them, and re-layouts: 2.75 us -> 2.07 us
    pallas_call x1, Pallas kernels: 15.8 us -> 13.3 us  [local(): pl.pallas_call(functools.partial(gather_kernel, sizes), out_shape=jax.Sha...]
    pallas_call x1, Pallas kernels: 15.3 us -> 13.8 us  [local(): pl.pallas_call(functools.partial(spread_kernel, sizes), out_shape=pltpu.V...]
    pallas_call x1, Pallas kernels: 8.8 us -> 7.52 us  [local(): pl.pallas_call(functools.partial(deposit_kernel, sizes, tiles, unroll), o...]
    reshape x1 -> x0, local copies, waits for them, and re-layouts: 0.67 us -> none  [local(): source_tiles.reshape(blocks, listed)]
    unnamed x3 -> x15, local copies, waits for them, and re-layouts: 2.08 us -> 2.07 us
where the time goes in v1:
time: 38 us; the launch traced here: 37.4 us
  Pallas kernels  34.6 us (91%)
  local copies, waits for them, and re-layouts  2.07 us (5%)
  between operations  0.74 us (2%)
    pallas_call x1, Pallas kernels, local(): pl.pallas_call(functools.partial(spread_kernel, sizes), out_shape=pltpu.V...  13.8 us
    pallas_call x1, Pallas kernels, local(): pl.pallas_call(functools.partial(gather_kernel, sizes), out_shape=jax.Sha...  13.3 us
    pallas_call x1, Pallas kernels, local(): pl.pallas_call(functools.partial(deposit_kernel, sizes, tiles, unroll), o...  7.52 us
    unnamed x15, local copies, waits for them, and re-layouts  2.07 us

profile of v1, /device:TPU:0, one launch (start us, length us, event | category | flops | bytes accessed | tf_op | source)
XLA Modules:
  0.0 37.4 jit_solution(15411207161180043788)
XLA Ops:
  0.7 0.0 copy-start.4
  0.7 0.7 %copy-done.4 = f32[1,1,1,2048]{3,2,1,0:T(1,128)S(1)} copy-done((f32[1,1,1,2048]{3,2,1,0:T(1,128)S(1)}, f32[1,1,1,2048]{3,2,1,0:T(1,128)}, u32[]{:S(2)}) %copy-start.4) | copy-done | bytes 8216
  1.4 0.0 copy-start
  1.4 0.7 %copy-done = f32[3,1,1,1,2048]{4,3,2,1,0:T(1,128)S(1)} copy-done((f32[3,1,1,1,2048]{4,3,2,1,0:T(1,128)S(1)}, f32[3,1,1,1,2048]{4,3,2,1,0:T(1,128)}, u32[]{:S(2)}) %copy-start) | copy-done | bytes 24600
  2.1 0.0 copy-start.1
  2.1 0.0 copy-start.2
  2.1 0.0 copy-start.3
  2.1 0.0 copy-start.5
  2.1 0.0 copy-start.6
  2.1 13.8 %shard_map.82.near = f32[18,4,16,128]{3,2,1,0:T(8,128)S(1)} custom-call(f32[3,16,128]{2,1,0:T(8,128)S(1)} %bitcast.13, f32[1,16,128]{2,1,0:T(8,128)S(1)} %bitcast.17), custom_call_target="tpu_custom_call" | custom-call | tf_op jit(solution)/shard_map/pallas_call | solution.py:258
  15.9 0.0 copy-done.1
  15.9 0.0 copy-done.2
  15.9 0.0 copy-done.3
  15.9 0.0 copy-done.5
  15.9 0.0 copy-done.6
  15.9 7.5 %shard_map.83.moved = f32[18,5,16,128]{3,2,1,0:T(8,128)S(1)} custom-call(s32[8,16]{1,0:T(8,128)S(1)} %bitcast.19, s32[1]{0:T(128)} %bitcast.11.count, f32[18,4,16,128]{3,2,1,0:T(8,128)S(1)} %shard_map.82.near, f32[3,16,128]{2,1,0:T(8,128)S(1)} %bitcast.14, f32[16,128]{1,0:T(8,128)S(1)} %bitcast.18, f32[2,16,128]{2,1,0:T(8,128)S(1)} %bitcast.16, ...), custom_call_target="tpu_custom_call" | custom-call | tf_op jit(solution)/shard_map/pallas_call | solution.py:272
  23.4 13.3 %shard_map.84 = f32[5,16,128]{2,1,0:T(8,128)S(1)} custom-call(f32[18,5,16,128]{3,2,1,0:T(8,128)S(1)} %shard_map.83.moved), custom_call_target="tpu_custom_call" | custom-call | tf_op jit(solution)/shard_map/pallas_call | solution.py:290
  36.8 0.6 %copy.13 = f32[5,1,1,1,2048]{4,3,2,1,0:T(1,128)} copy(f32[5,1,1,1,2048]{4,3,2,1,0:T(1,128)S(1)} %bitcast.12) | data formatting | bytes 81920
Async XLA Ops:
  0.7 0.7 %copy-start.4 = (f32[1,1,1,2048]{3,2,1,0:T(1,128)S(1)}, f32[1,1,1,2048]{3,2,1,0:T(1,128)}, u32[]{:S(2)}) copy-start(f32[1,1,1,2048]{3,2,1,0:T(1,128)} %param.9) | copy-start | bytes 24580
  1.4 0.7 %copy-start = (f32[3,1,1,1,2048]{4,3,2,1,0:T(1,128)S(1)}, f32[3,1,1,1,2048]{4,3,2,1,0:T(1,128)}, u32[]{:S(2)}) copy-start(f32[3,1,1,1,2048]{4,3,2,1,0:T(1,128)} %param.8) | copy-start | bytes 73732
  2.1 13.8 %copy-start.1 = (f32[3,1,1,1,2048]{4,3,2,1,0:T(1,128)S(1)}, f32[3,1,1,1,2048]{4,3,2,1,0:T(1,128)}, u32[]{:S(2)}) copy-start(f32[3,1,1,1,2048]{4,3,2,1,0:T(1,128)} %param.10) | copy-start | bytes 73732
  2.1 13.8 %copy-start.2 = (f32[3,1,1,1,2048]{4,3,2,1,0:T(1,128)S(1)}, f32[3,1,1,1,2048]{4,3,2,1,0:T(1,128)}, u32[]{:S(2)}) copy-start(f32[3,1,1,1,2048]{4,3,2,1,0:T(1,128)} %param.13) | copy-start | bytes 73732
  2.1 13.8 %copy-start.3 = (f32[2,1,1,1,2048]{4,3,2,1,0:T(1,128)S(1)}, f32[2,1,1,1,2048]{4,3,2,1,0:T(1,128)}, u32[]{:S(2)}) copy-start(f32[2,1,1,1,2048]{4,3,2,1,0:T(1,128)} %param.12) | copy-start | bytes 49156
  2.1 13.8 %copy-start.5 = (f32[1,1,1,2048]{3,2,1,0:T(1,128)S(1)}, f32[1,1,1,2048]{3,2,1,0:T(1,128)}, u32[]{:S(2)}) copy-start(f32[1,1,1,2048]{3,2,1,0:T(1,128)} %param.11) | copy-start | bytes 24580
  2.1 13.8 %copy-start.6 = (s32[1,1,1,16,8]{3,4,2,1,0:T(8,128)S(1)}, s32[1,1,1,16,8]{3,4,2,1,0:T(8,128)}, u32[]{:S(2)}) copy-start(s32[1,1,1,16,8]{3,4,2,1,0:T(8,128)} %param.14) | copy-start | bytes 1540
